TPU v7x, 32 devices: a whole 2x2x4 slice. The times are simulated.
32 devices in a mesh: row: 2 (over x), col: 4 (over z), depth: 4 (over y, core).
Axes of the slice: x: 2, y: 2, z: 4, core: 2. Of those that a mesh axis runs over, the one named last changes fastest.
Arguments:
- pair: bfloat16 [768, 768, 128], P('row', 'col'), may hold values from -6 to 6
- ln_gain: float32 [128], replicated, may hold values from 0.1 to 1.9
- ln_shift: float32 [128], replicated, may hold values from -3 to 3
- proj_weight: bfloat16 [128, 512], replicated, may hold values from -0.5 to 0.5
- proj_bias: float32 [512], replicated, may hold values from -3 to 3
- gate_weight: bfloat16 [128, 128], replicated, may hold values from -0.5 to 0.5
- gate_bias: float32 [128], replicated, may hold values from -3 to 3
- out_gain: float32 [128], replicated, may hold values from 0.1 to 1.9
- out_shift: float32 [128], replicated, may hold values from -3 to 3
- out_weight: bfloat16 [128, 128], replicated, may hold values from -0.5 to 0.5
- out_bias: float32 [128], replicated, may hold values from -3 to 3
Outputs:
- update: bfloat16 [768, 768, 128], P('row', 'col')
All inputs are finite; a program needn't handle non-finite values.
Results may differ from a plain program's by a relative error of at most 0.0051.
Values may be sent and summed in bfloat16 or wider, within the bound.
No kernel may reach another device: no remote copies, remote signals or barrier semaphores. Data moves between devices by JAX's collectives and lax.ppermute only.
A program may use at most 256 MiB of HBM per device.

v0:
```python
import jax
import jax.numpy as jnp
from jax import lax
from jax.sharding import PartitionSpec as P


def layer_norm(values, gain, shift):
    centre = jnp.mean(values, axis=-1, keepdims=True)
    centred = values - centre
    spread = jnp.mean(centred * centred, axis=-1, keepdims=True)
    return centred * lax.rsqrt(spread + 1e-05) * gain + shift


def project(piece, ln_gain, ln_shift, proj_weight, proj_bias, gate_weight, gate_bias):
    hidden = proj_weight.shape[1] // 4
    channels = piece.shape[2]
    normed = layer_norm(piece.astype(jnp.float32), ln_gain, ln_shift).astype(jnp.bfloat16)
    flat = normed.reshape(-1, channels)
    mixed = jnp.dot(flat, proj_weight, preferred_element_type=jnp.float32) + proj_bias
    left = (jax.nn.sigmoid(mixed[:, :hidden]) * mixed[:, hidden : 2 * hidden]).astype(jnp.bfloat16)
    right = (jax.nn.sigmoid(mixed[:, 2 * hidden : 3 * hidden]) * mixed[:, 3 * hidden :]).astype(
        jnp.bfloat16
    )
    gate = jax.nn.sigmoid(
        jnp.dot(flat, gate_weight, preferred_element_type=jnp.float32) + gate_bias
    )
    shape = (piece.shape[0], piece.shape[1])
    return (
        left.reshape(shape + (hidden,)),
        right.reshape(shape + (hidden,)),
        gate.reshape(shape + (channels,)),
    )


def finish(triangle, gate, out_gain, out_shift, out_weight, out_bias):
    hidden = triangle.shape[2]
    tri_normed = layer_norm(triangle, out_gain, out_shift).astype(jnp.bfloat16)
    projected = (
        jnp.dot(tri_normed.reshape(-1, hidden), out_weight, preferred_element_type=jnp.float32)
        + out_bias
    )
    return (gate * projected.reshape(gate.shape)).astype(jnp.bfloat16)


def per_device(
    pair,
    ln_gain,
    ln_shift,
    proj_weight,
    proj_bias,
    gate_weight,
    gate_bias,
    out_gain,
    out_shift,
    out_weight,
    out_bias,
):
    depth_count = lax.axis_size("depth")
    depth_id = lax.axis_index("depth")
    cols_here = pair.shape[1]
    quarter = cols_here // depth_count
    piece = lax.dynamic_slice_in_dim(pair, depth_id * quarter, quarter, 1)
    left, right, gate = project(
        piece, ln_gain, ln_shift, proj_weight, proj_bias, gate_weight, gate_bias
    )
    left_all = lax.all_gather(left, ("col", "depth"), axis=1, tiled=True)
    right_column = lax.all_gather(right, "row", axis=0, tiled=True)
    needed = lax.all_to_all(right_column, ("col", "depth"), split_axis=0, concat_axis=1, tiled=True)
    triangle = jnp.einsum("ikc,jkc->ijc", left_all, needed, preferred_element_type=jnp.float32)
    finished = finish(triangle, gate, out_gain, out_shift, out_weight, out_bias)
    return lax.all_gather(finished, "depth", axis=1, tiled=True)


def solution(mesh):
    placed = (P("row", "col", None), P(), P(), P(), P(), P(), P(), P(), P(), P(), P())
    return jax.shard_map(
        per_device, mesh=mesh, in_specs=placed, out_specs=P("row", "col", None), check_vma=False
    )
```

profile of v0, /device:TPU:0, one launch (start us, length us, event | category | flops | bytes accessed | tf_op | source)
XLA Modules:
  0.0 949.2 jit_solution(18416673488483238151)
XLA Ops:
  6.6 4.9 convert_reduce_fusion
  11.6 0.1 copy.42
  11.8 7.2 fusion.8
  19.1 0.1 copy.44
  19.2 7.0 fusion.11
  26.3 14.7 %convolution_add_fusion = f32[18432,512]{1,0:T(8,128)} fusion(bf16[18432,128]{1,0:T(8,128)(2,1)S(1)} %bitcast.27, bf16[128,512]{1,0:T(8,128)(2,1)S(1)} %copy-done, f32[512]{0:T(512)S(1)} %copy-done.5), kind=kOutput, calls=%fused_computation | convolution fusion | flops 2425356288 | bytes 42600448 | tf_op jit(solution)/shard_map/dot_general | solution.py:19
  41.0 17.7 %fusion.12 = (bf16[18432,128]{1,0:T(8,128)(2,1)}, bf16[18432,128]{1,0:T(8,128)(2,1)}) fusion(f32[18432,512]{1,0:T(8,128)} %convolution_add_fusion), kind=kLoop, calls=%fused_computation.18 | loop fusion | flops 23592960 | bytes 47185920 | tf_op jit(solution)/shard_map/convert_element_type | solution.py:20
  58.9 7.6 copy.46
  66.5 113.2 %all-gather.4.cloned.1.call-done = bf16[768,48,128]{2,1,0:T(8,128)(2,1)} async-done(((bf16[384,48,128]{2,1,0:T(8,128)(2,1)}), bf16[768,48,128]{2,1,0:T(8,128)(2,1)}) %all-gather.4.cloned.1.call-update) | async-done | bytes 9437200 | tf_op jit(solution)/shard_map/all_gather | solution.py:67
  179.7 5.7 all-to-all-start
  185.3 0.2 all-gather.8.cloned.1.call-start
  185.6 8.9 fusion.5
  194.4 299.5 %all-to-all-done = bf16[768,48,128]{2,1,0:T(8,128)(2,1)} async-done(((bf16[768,48,128]{2,1,0:T(8,128)(2,1)}), bf16[768,48,128]{2,1,0:T(8,128)(2,1)}, u32[]{:S(2)}, u32[]{:S(2)}) %all-to-all-start) | async-done | bytes 9437216 | tf_op jit(solution)/shard_map/all_to_all | solution.py:68
  493.9 10.1 %copy.45 = bf16[48,16,48,128]{3,2,1,0:T(8,128)(2,1)} copy(bf16[48,16,48,128]{3,2,0,1:T(8,128)(2,1)} %bitcast.3) | data formatting | bytes 18874368 | tf_op jit(solution)/shard_map/all_to_all | solution.py:68
  504.0 13.3 %copy.47 = bf16[48,768,128]{1,0,2:T(8,128)(2,1)} copy(bf16[48,768,128]{2,1,0:T(8,128)(2,1)} %bitcast.24) | data formatting | bytes 18874368 | tf_op jit(solution)/shard_map/all_to_all | solution.py:68
  517.2 195.3 %all-gather.6.cloned.1.call-done = bf16[384,768,128]{0,1,2:T(8,128)(2,1)} async-done(((bf16[384,48,128]{0,1,2:T(8,128)(2,1)}), bf16[384,768,128]{0,1,2:T(8,128)(2,1)}) %all-gather.6.cloned.1.call-update) | async-done | bytes 75497488 | tf_op jit(solution)/shard_map/all_gather | solution.py:66
  712.6 32.4 %bitcast_reduce_fusion = (f32[384,48]{0,1:T(8,128)S(1)}, f32[128,48,384]{2,1,0:T(8,128)}) fusion(bf16[48,768,128]{1,0,2:T(8,128)(2,1)} %copy.47, bf16[384,768,128]{0,1,2:T(8,128)(2,1)} %all-gather.6.cloned.1.call-done), kind=kOutput, calls=%fused_computation.30 | convolution fusion | flops 3626219520 | bytes 94445568 | tf_op jit(solution)/shard_map/ikc,jkc->ijc/dot_general | solution.py:69
  745.0 4.8 multiply_reduce_fusion
  749.9 1.5 copy-done.2
  751.4 3.8 add_convert_fusion
  755.2 7.5 copy.48
  762.7 8.7 fusion.4
  771.5 153.4 %all-gather.8.cloned.1.call-done = bf16[384,192,128]{2,1,0:T(8,128)(2,1)} async-done(((bf16[384,48,128]{2,1,0:T(8,128)(2,1)}), bf16[384,192,128]{2,1,0:T(8,128)(2,1)}) %all-gather.8.cloned.1.call-update) | async-done | bytes 18874384 | tf_op jit(solution)/shard_map/all_gather | solution.py:71
  924.9 17.8 %copy.50 = bf16[384,192,128]{2,1,0:T(8,128)(2,1)} copy(bf16[384,192,128]{2,1,0:T(8,128)(2,1)} %all-gather.8.cloned.1.call-done) | data formatting | bytes 37748736
  (36 shorter events, 0.4 us)
Async XLA Ops:
  6.5 19.8 %copy-start = (bf16[128,512]{1,0:T(8,128)(2,1)S(1)}, bf16[128,512]{1,0:T(8,128)(2,1)}, u32[]{:S(2)}) copy-start(bf16[128,512]{1,0:T(8,128)(2,1)} %param.14) | copy-start | bytes 393220
  6.5 12.7 %copy-start.10 = (f32[128]{0:T(128)S(1)}, f32[128]{0:T(128)}, u32[]{:S(2)}) copy-start(f32[128]{0:T(128)} %param.12) | copy-start | bytes 1540
  6.5 12.7 %copy-start.9 = (f32[128]{0:T(128)S(1)}, f32[128]{0:T(128)}, u32[]{:S(2)}) copy-start(f32[128]{0:T(128)} %param.13) | copy-start | bytes 1540
  6.5 173.1 %all-gather.4.cloned.1.call-start = ((), (), s32[]{:S(2)}) async-start(), calls=%async_computation.1 | async-start | bytes 14155776 | tf_op jit(solution)/shard_map/all_gather | solution.py:67
  6.6 19.7 %copy-start.5 = (f32[512]{0:T(512)S(1)}, f32[512]{0:T(512)}, u32[]{:S(2)}) copy-start(f32[512]{0:T(512)} %param.15) | copy-start | bytes 6148
  26.3 14.8 %copy-start.3 = (bf16[384,48,128]{2,1,0:T(8,128)(2,1)}, bf16[384,48,128]{2,1,0:T(8,128)(2,1)S(1)}, u32[]{:S(2)}) copy-start(bf16[384,48,128]{2,1,0:T(8,128)(2,1)S(1)} %fusion.11) | copy-start | bytes 14155780
  58.8 653.8 %all-gather.6.cloned.1.call-start = ((), (), s32[]{:S(2)}) async-start(), calls=%async_computation.2 | async-start | bytes 80216064 | tf_op jit(solution)/shard_map/all_gather | solution.py:66
  66.5 119.1 %copy-start.11 = (bf16[128,128]{1,0:T(8,128)(2,1)S(1)}, bf16[128,128]{1,0:T(8,128)(2,1)}, u32[]{:S(2)}) copy-start(bf16[128,128]{1,0:T(8,128)(2,1)} %param.16) | copy-start | bytes 98308
  66.5 119.1 %copy-start.12 = (f32[128]{0:T(128)S(1)}, f32[128]{0:T(128)}, u32[]{:S(2)}) copy-start(f32[128]{0:T(128)} %param.17) | copy-start | bytes 1540
  179.7 314.3 %all-to-all-start = ((bf16[768,48,128]{2,1,0:T(8,128)(2,1)}), bf16[768,48,128]{2,1,0:T(8,128)(2,1)}, u32[]{:S(2)}, u32[]{:S(2)}) async-start(bf16[768,48,128]{2,1,0:T(8,128)(2,1)} %all-gather.4.cloned.1.call-done), calls=%async_computation | async-start | bytes 18874368 | tf_op jit(solution)/shard_map/all_to_all | solution.py:68
  185.3 739.5 %all-gather.8.cloned.1.call-start = ((), (), s32[]{:S(2)}) async-start(), calls=%async_computation.3 | async-start | bytes 23592960 | tf_op jit(solution)/shard_map/all_gather | solution.py:71
  745.0 6.4 copy-start.2
  745.0 6.4 copy-start.7
  745.0 6.4 copy-start.8
  751.4 11.3 %copy-start.4 = (bf16[128,128]{1,0:T(8,128)(2,1)S(1)}, bf16[128,128]{1,0:T(8,128)(2,1)}, u32[]{:S(2)}) copy-start(bf16[128,128]{1,0:T(8,128)(2,1)} %param.20) | copy-start | bytes 98308
  751.4 11.3 %copy-start.6 = (f32[128]{0:T(128)S(1)}, f32[128]{0:T(128)}, u32[]{:S(2)}) copy-start(f32[128]{0:T(128)} %param.21) | copy-start | bytes 1540
  924.9 17.8 %copy-start.1 = (bf16[128,512]{1,0:T(8,128)(2,1)S(1)}, bf16[128,512]{1,0:T(8,128)(2,1)}, u32[]{:S(2)}) copy-start(bf16[128,512]{1,0:T(8,128)(2,1)} %param.14) | copy-start | bytes 393220
Sparse Core Ops, SparseCore 0:
  58.9 120.6 all-gather.3
  181.2 531.3 all-gather.5
  771.6 153.2 all-gather.7
where the time goes:
time: 950 us; the launch traced here: 949 us
  waiting for transfers between devices  761 us (80%)
  matrix products  64.7 us (7%)
  local copies, waits for them, and re-layouts  58.2 us (6%)
  other arithmetic  45.6 us (5%)
  between operations  13.3 us (1%)
    all_to_all x1, waiting for transfers between devices, per_device(): lax.all_to_all(right_column, ('col', 'depth'), split_axis=0, concat_axis=...  299 us
    all_gather x1, waiting for transfers between devices, per_device(): left_all = lax.all_gather(left, ('col', 'depth'), axis=1, tiled=True)  195 us
    all_gather x1, waiting for transfers between devices, per_device(): return lax.all_gather(finished, 'depth', axis=1, tiled=True)  153 us
    all_gather x1, waiting for transfers between devices, per_device(): right_column = lax.all_gather(right, 'row', axis=0, tiled=True)  113 us
    dot_general x1, matrix products, per_device(): jnp.einsum('ikc,jkc->ijc', left_all, needed, preferred_element_type=jnp.f...  32.4 us
    all_to_all x2, local copies, waits for them, and re-layouts, per_device(): lax.all_to_all(right_column, ('col', 'depth'), split_axis=0, concat_axis=...  23.3 us
    unnamed x27, local copies, waits for them, and re-layouts  19.3 us
  transfers between devices with their start and end apart: 4, of which 4 were waited for; matrix products, arithmetic and copies ran while one was open for 4% of the time, Pallas kernels for 0%

commit v1 on v0

--- a/solution.py
+++ b/solution.py
@@ -63,10 +63,44 @@
     left, right, gate = project(
         piece, ln_gain, ln_shift, proj_weight, proj_bias, gate_weight, gate_bias
     )
-    left_all = lax.all_gather(left, ("col", "depth"), axis=1, tiled=True)
     right_column = lax.all_gather(right, "row", axis=0, tiled=True)
     needed = lax.all_to_all(right_column, ("col", "depth"), split_axis=0, concat_axis=1, tiled=True)
-    triangle = jnp.einsum("ikc,jkc->ijc", left_all, needed, preferred_element_type=jnp.float32)
+    size, index, extent = (
+        lax.axis_size(("col", "depth")),
+        lax.axis_index(("col", "depth")),
+        left.shape[1],
+    )
+    right_2 = [(i, (i + 1) % size) for i in range(size)]
+    backward = [(i, (i - 1) % size) for i in range(size)]
+    half = size // 2
+    from_left = from_right = left
+    total = jnp.einsum(
+        "ikc,jkc->ijc",
+        left,
+        lax.dynamic_slice_in_dim(needed, index * extent, left.shape[1], axis=1),
+        preferred_element_type=jnp.float32,
+    )
+    for step in range(1, half + 1):
+        from_left = lax.ppermute(from_left, ("col", "depth"), right_2)
+        if step < size - half:
+            from_right = lax.ppermute(from_right, ("col", "depth"), backward)
+            total = total + jnp.einsum(
+                "ikc,jkc->ijc",
+                from_right,
+                lax.dynamic_slice_in_dim(
+                    needed, (index + step) % size * extent, from_right.shape[1], axis=1
+                ),
+                preferred_element_type=jnp.float32,
+            )
+        total = total + jnp.einsum(
+            "ikc,jkc->ijc",
+            from_left,
+            lax.dynamic_slice_in_dim(
+                needed, (index - step) % size * extent, from_left.shape[1], axis=1
+            ),
+            preferred_element_type=jnp.float32,
+        )
+    triangle = total
     finished = finish(triangle, gate, out_gain, out_shift, out_weight, out_bias)
     return lax.all_gather(finished, "depth", axis=1, tiled=True)
 

time: 950 us -> 1240 us (1.31)
  starting transfers between devices: 5.93 us -> 554 us
  waiting for transfers between devices: 761 us -> 337 us
  matrix products: 64.7 us -> 190 us
  local copies, waits for them, and re-layouts: 58.2 us -> 93.4 us
    ppermute x0 -> x15, starting transfers between devices: none -> 548 us  [the longest x8 531 us: per_device(): from_left = lax.ppermute(from_left, ('col', 'depth'), right_2)]
    all_to_all x1, waiting for transfers between devices: 299 us -> 0.01 us  [per_device(): lax.all_to_all(right_column, ('col', 'depth'), split_axis=0, concat_axis=...]
    all_gather x1 -> x0, waiting for transfers between devices: 195 us -> none  [per_device(): left_all = lax.all_gather(left, ('col', 'depth'), axis=1, tiled=True)]
    ppermute x0 -> x15, waiting for transfers between devices: none -> 170 us  [the longest x7 92.6 us: per_device(): from_right = lax.ppermute(from_right, ('col', 'depth'), backward)]
    dot_general x1 -> x16, matrix products: 32.4 us -> 158 us  [the longest x8 101 us: per_device(): jnp.einsum('ikc,jkc->ijc', from_left, lax.dynamic_slice_in_dim(needed, (i...]
    all_gather x1, waiting for transfers between devices: 113 us -> 0.01 us  [per_device(): right_column = lax.all_gather(right, 'row', axis=0, tiled=True)]
    unnamed x27 -> x87, local copies, waits for them, and re-layouts: 19.3 us -> 60.4 us
    all_gather x1, waiting for transfers between devices: 153 us -> 167 us  [per_device(): return lax.all_gather(finished, 'depth', axis=1, tiled=True)]
  transfers between devices with their start and end apart: 4 -> 18, of which waited for: 4 -> 6; matrix products, arithmetic and copies ran while one was open for 4% -> 14% of each run, Pallas kernels for 0% -> 0%
where the time goes in v1:
time: 1240 us; the launch traced here: 1230 us
  starting transfers between devices  554 us (45%)
  waiting for transfers between devices  337 us (27%)
  matrix products  190 us (15%)
  local copies, waits for them, and re-layouts  93.4 us (8%)
  other arithmetic  45.5 us (4%)
  between operations  13.9 us (1%)
    ppermute x8, starting transfers between devices, per_device(): from_left = lax.ppermute(from_left, ('col', 'depth'), right_2)  531 us
    all_gather x1, waiting for transfers between devices, per_device(): return lax.all_gather(finished, 'depth', axis=1, tiled=True)  167 us
    dot_general x8, matrix products, per_device(): jnp.einsum('ikc,jkc->ijc', from_left, lax.dynamic_slice_in_dim(needed, (i...  101 us
    ppermute x7, waiting for transfers between devices, per_device(): from_right = lax.ppermute(from_right, ('col', 'depth'), backward)  92.6 us
    ppermute x8, waiting for transfers between devices, per_device(): from_left = lax.ppermute(from_left, ('col', 'depth'), right_2)  77.5 us
    unnamed x87, local copies, waits for them, and re-layouts  60.4 us
    dot_general x7, matrix products, per_device(): jnp.einsum('ikc,jkc->ijc', from_right, lax.dynamic_slice_in_dim(needed, (...  47.8 us
  transfers between devices with their start and end apart: 18, of which 6 were waited for; matrix products, arithmetic and copies ran while one was open for 14% of the time, Pallas kernels for 0%

profile of v1, /device:TPU:0, one launch (start us, length us, event | category | flops | bytes accessed | tf_op | source)
XLA Modules:
  0.0 1233.7 jit_solution(14483596100839880992)
XLA Ops:
  26.3 14.8 %convolution_add_fusion = f32[18432,512]{1,0:T(8,128)} fusion(bf16[18432,128]{1,0:T(8,128)(2,1)S(1)} %bitcast.57, bf16[128,512]{1,0:T(8,128)(2,1)S(1)} %copy-done, f32[512]{0:T(512)S(1)} %copy-done.21), kind=kOutput, calls=%fused_computation | convolution fusion | flops 2425356288 | bytes 42600448 | tf_op jit(solution)/shard_map/dot_general | solution.py:19
  41.0 17.7 %fusion.12 = (bf16[18432,128]{1,0:T(8,128)(2,1)}, bf16[18432,128]{1,0:T(8,128)(2,1)}) fusion(f32[18432,512]{1,0:T(8,128)} %convolution_add_fusion), kind=kLoop, calls=%fused_computation.18 | loop fusion | flops 23592960 | bytes 47185920 | tf_op jit(solution)/shard_map/convert_element_type | solution.py:20
  71.9 52.1 %collective-permute-done.1 = bf16[384,48,128]{0,1,2:T(8,128)(2,1)} collective-permute-done((bf16[384,48,128]{0,1,2:T(8,128)(2,1)}, bf16[384,48,128]{0,1,2:T(8,128)(2,1)}, u32[]{:S(2)}, u32[]{:S(2)}) %collective-permute-start.1) | collective-permute-done | bytes 4718624 | tf_op jit(solution)/shard_map/ppermute | solution.py:84
  124.1 47.4 %collective-permute-start.3 = (bf16[384,48,128]{0,1,2:T(8,128)(2,1)}, bf16[384,48,128]{0,1,2:T(8,128)(2,1)}, u32[]{:S(2)}, u32[]{:S(2)}) collective-permute-start(bf16[384,48,128]{0,1,2:T(8,128)(2,1)} %collective-permute-done.1), channel_id=1, source_target_pairs={{0,1},{1,2},{2,3},{3,4},{4,5},{5,6},{6,7},{7,8},{8,9},{9,10},{10,1... | collective-permute-start | bytes 14155784 | tf_op jit(solution)/shard_map/ppermute | solution.py:84
  171.4 9.3 collective-permute-done.3
  180.7 94.4 %collective-permute-start.5 = (bf16[384,48,128]{0,1,2:T(8,128)(2,1)}, bf16[384,48,128]{0,1,2:T(8,128)(2,1)}, u32[]{:S(2)}, u32[]{:S(2)}) collective-permute-start(bf16[384,48,128]{0,1,2:T(8,128)(2,1)} %collective-permute-done.3), channel_id=1, source_target_pairs={{0,1},{1,2},{2,3},{3,4},{4,5},{5,6},{6,7},{7,8},{8,9},{9,10},{10,1... | collective-permute-start | bytes 14155784 | tf_op jit(solution)/shard_map/ppermute | solution.py:84
  285.6 106.8 %collective-permute-start.7 = (bf16[384,48,128]{0,1,2:T(8,128)(2,1)}, bf16[384,48,128]{0,1,2:T(8,128)(2,1)S(1)}, u32[]{:S(2)}, u32[]{:S(2)}) collective-permute-start(bf16[384,48,128]{0,1,2:T(8,128)(2,1)} %collective-permute-done.5), channel_id=1, source_target_pairs={{0,1},{1,2},{2,3},{3,4},{4,5},{5,6},{6,7},{7,8},{8,9},{9,10},{10,1... | collective-permute-start | bytes 14155784 | tf_op jit(solution)/shard_map/ppermute | solution.py:84
  392.4 92.6 %collective-permute-done.4 = bf16[384,48,128]{0,1,2:T(8,128)(2,1)S(1)} collective-permute-done((bf16[384,48,128]{0,1,2:T(8,128)(2,1)}, bf16[384,48,128]{0,1,2:T(8,128)(2,1)S(1)}, u32[]{:S(2)}, u32[]{:S(2)}) %collective-permute-start.4) | collective-permute-done | bytes 4718624 | tf_op jit(solution)/shard_map/ppermute | solution.py:86
  491.9 140.5 %collective-permute-start.9 = (bf16[384,48,128]{0,1,2:T(8,128)(2,1)S(1)}, bf16[384,48,128]{0,1,2:T(8,128)(2,1)}, u32[]{:S(2)}, u32[]{:S(2)}) collective-permute-start(bf16[384,48,128]{0,1,2:T(8,128)(2,1)S(1)} %collective-permute-done.7), channel_id=1, source_target_pairs={{0,1},{1,2},{2,3},{3,4},{4,5},{5,6},{6,7},{7,8},{8,9},{9,10},{10,1... | collective-permute-start | bytes 14155784 | tf_op jit(solution)/shard_map/ppermute | solution.py:84
  640.0 45.8 %collective-permute-start.11 = (bf16[384,48,128]{0,1,2:T(8,128)(2,1)}, bf16[384,48,128]{0,1,2:T(8,128)(2,1)}, u32[]{:S(2)}, u32[]{:S(2)}) collective-permute-start(bf16[384,48,128]{0,1,2:T(8,128)(2,1)} %collective-permute-done.9), channel_id=1, source_target_pairs={{0,1},{1,2},{2,3},{3,4},{4,5},{5,6},{6,7},{7,8},{8,9},{9,10},{10,1... | collective-permute-start | bytes 14155784 | tf_op jit(solution)/shard_map/ppermute | solution.py:84
  689.0 8.7 fusion.5
  697.7 92.6 %collective-permute-start.13 = (bf16[384,48,128]{0,1,2:T(8,128)(2,1)}, bf16[384,48,128]{0,1,2:T(8,128)(2,1)}, u32[]{:S(2)}, u32[]{:S(2)}) collective-permute-start(bf16[384,48,128]{0,1,2:T(8,128)(2,1)} %collective-permute-done.11), channel_id=1, source_target_pairs={{0,1},{1,2},{2,3},{3,4},{4,5},{5,6},{6,7},{7,8},{8,9},{9,10},{10,1... | collective-permute-start | bytes 14155784 | tf_op jit(solution)/shard_map/ppermute | solution.py:84
  790.3 10.1 copy.115
  846.6 8.4 fusion.20
  855.0 7.9 fusion.29
  862.9 7.9 fusion.30
  905.5 7.9 fusion.24
  913.5 7.9 fusion.21
  929.2 7.8 fusion.31
  958.0 8.5 collective-permute-done.14
  966.5 49.2 %bitcast_reduce_fusion = (f32[384,48]{0,1:T(8,128)S(1)}, f32[128,48,384]{2,1,0:T(8,128)}) fusion(bf16[48,48,128]{1,0,2:T(8,128)(2,1)S(1)} %copy.151, bf16[384,48,128]{0,1,2:T(8,128)(2,1)} %collective-permute-done.14, f32[128,48,384]{2,1,0:T(8,128)} %fusion.34, f32[128,48,384]{2,1,0:T(8,128)} %fusion.33, f32[128,48,384]{2,1,0:T(8,128)} %fusion.32, ...), kind=kOutput, calls=%fused_computation.30 | convolution fusion | flops 264222720 | bytes 156377088 | tf_op jit(solution)/shard_map/ikc,jkc->ijc/dot_general | solution.py:95
  1033.5 8.6 fusion.4
  1042.2 166.7 %all-gather.5.cloned.1.call-done = bf16[384,192,128]{2,1,0:T(8,128)(2,1)} async-done(((bf16[384,48,128]{2,1,0:T(8,128)(2,1)}), bf16[384,192,128]{2,1,0:T(8,128)(2,1)}) %all-gather.5.cloned.1.call-update) | async-done | bytes 18874384 | tf_op jit(solution)/shard_map/all_gather | solution.py:105
  1208.9 17.8 %copy.153 = bf16[384,192,128]{2,1,0:T(8,128)(2,1)} copy(bf16[384,192,128]{2,1,0:T(8,128)(2,1)} %all-gather.5.cloned.1.call-done) | data formatting | bytes 37748736
  (141 shorter events, 188.4 us)
Async XLA Ops:
  6.5 19.7 %copy-start = (bf16[128,512]{1,0:T(8,128)(2,1)S(1)}, bf16[128,512]{1,0:T(8,128)(2,1)}, u32[]{:S(2)}) copy-start(bf16[128,512]{1,0:T(8,128)(2,1)} %param.14) | copy-start | bytes 393220
  6.5 268.6 %all-gather.3.cloned.1.call-start = ((), (), s32[]{:S(2)}) async-start(), calls=%async_computation.1 | async-start | bytes 14155776 | tf_op jit(solution)/shard_map/all_gather | solution.py:66
  66.4 57.7 %collective-permute-start.1 = (bf16[384,48,128]{0,1,2:T(8,128)(2,1)}, bf16[384,48,128]{0,1,2:T(8,128)(2,1)}, u32[]{:S(2)}, u32[]{:S(2)}) collective-permute-start(bf16[384,48,128]{0,1,2:T(8,128)(2,1)} %copy.117), channel_id=1, source_target_pairs={{0,1},{1,2},{2,3},{3,4},{4,5},{5,6},{6,7},{7,8},{8,9},{9,10},{10,1... | collective-permute-start | bytes 14155784 | tf_op jit(solution)/shard_map/ppermute | solution.py:84
  66.9 622.1 %copy-start.27 = (bf16[128,128]{1,0:T(8,128)(2,1)S(1)}, bf16[128,128]{1,0:T(8,128)(2,1)}, u32[]{:S(2)}) copy-start(bf16[128,128]{1,0:T(8,128)(2,1)} %param.16) | copy-start | bytes 98308
  66.9 622.1 %copy-start.28 = (f32[128]{0:T(128)S(1)}, f32[128]{0:T(128)}, u32[]{:S(2)}) copy-start(f32[128]{0:T(128)} %param.17) | copy-start | bytes 1540
  66.9 104.5 %collective-permute-start = (bf16[384,48,128]{0,1,2:T(8,128)(2,1)}, bf16[384,48,128]{0,1,2:T(8,128)(2,1)}, u32[]{:S(2)}, u32[]{:S(2)}) collective-permute-start(bf16[384,48,128]{0,1,2:T(8,128)(2,1)} %copy.117), channel_id=1, source_target_pairs={{0,15},{1,0},{2,1},{3,2},{4,3},{5,4},{6,5},{7,6},{8,7},{9,8},{10,9... | collective-permute-start | bytes 14155784 | tf_op jit(solution)/shard_map/ppermute | solution.py:86
  124.1 56.7 %collective-permute-start.3 = (bf16[384,48,128]{0,1,2:T(8,128)(2,1)}, bf16[384,48,128]{0,1,2:T(8,128)(2,1)}, u32[]{:S(2)}, u32[]{:S(2)}) collective-permute-start(bf16[384,48,128]{0,1,2:T(8,128)(2,1)} %collective-permute-done.1), channel_id=1, source_target_pairs={{0,1},{1,2},{2,3},{3,4},{4,5},{5,6},{6,7},{7,8},{8,9},{9,10},{10,1... | collective-permute-start | bytes 14155784 | tf_op jit(solution)/shard_map/ppermute | solution.py:84
  171.4 109.8 %collective-permute-start.2 = (bf16[384,48,128]{0,1,2:T(8,128)(2,1)}, bf16[384,48,128]{0,1,2:T(8,128)(2,1)}, u32[]{:S(2)}, u32[]{:S(2)}) collective-permute-start(bf16[384,48,128]{0,1,2:T(8,128)(2,1)} %collective-permute-done), channel_id=1, source_target_pairs={{0,15},{1,0},{2,1},{3,2},{4,3},{5,4},{6,5},{7,6},{8,7},{9,8},{10,9... | collective-permute-start | bytes 14155784 | tf_op jit(solution)/shard_map/ppermute | solution.py:86
  180.7 104.9 %collective-permute-start.5 = (bf16[384,48,128]{0,1,2:T(8,128)(2,1)}, bf16[384,48,128]{0,1,2:T(8,128)(2,1)}, u32[]{:S(2)}, u32[]{:S(2)}) collective-permute-start(bf16[384,48,128]{0,1,2:T(8,128)(2,1)} %collective-permute-done.3), channel_id=1, source_target_pairs={{0,1},{1,2},{2,3},{3,4},{4,5},{5,6},{6,7},{7,8},{8,9},{9,10},{10,1... | collective-permute-start | bytes 14155784 | tf_op jit(solution)/shard_map/ppermute | solution.py:84
  275.1 515.2 %all-to-all-start = ((bf16[768,48,128]{2,1,0:T(8,128)(2,1)}), bf16[768,48,128]{2,1,0:T(8,128)(2,1)}, u32[]{:S(2)}, u32[]{:S(2)}) async-start(bf16[768,48,128]{2,1,0:T(8,128)(2,1)} %all-gather.3.cloned.1.call-done), calls=%async_computation | async-start | bytes 18874368 | tf_op jit(solution)/shard_map/all_to_all | solution.py:67
  281.2 927.7 %all-gather.5.cloned.1.call-start = ((), (), s32[]{:S(2)}) async-start(), calls=%async_computation.2 | async-start | bytes 23592960 | tf_op jit(solution)/shard_map/all_gather | solution.py:105
  281.3 203.8 %collective-permute-start.4 = (bf16[384,48,128]{0,1,2:T(8,128)(2,1)}, bf16[384,48,128]{0,1,2:T(8,128)(2,1)S(1)}, u32[]{:S(2)}, u32[]{:S(2)}) collective-permute-start(bf16[384,48,128]{0,1,2:T(8,128)(2,1)} %collective-permute-done.2), channel_id=1, source_target_pairs={{0,15},{1,0},{2,1},{3,2},{4,3},{5,4},{6,5},{7,6},{8,7},{9,8},{10,9... | collective-permute-start | bytes 14155784 | tf_op jit(solution)/shard_map/ppermute | solution.py:86
  285.6 206.2 %collective-permute-start.7 = (bf16[384,48,128]{0,1,2:T(8,128)(2,1)}, bf16[384,48,128]{0,1,2:T(8,128)(2,1)S(1)}, u32[]{:S(2)}, u32[]{:S(2)}) collective-permute-start(bf16[384,48,128]{0,1,2:T(8,128)(2,1)} %collective-permute-done.5), channel_id=1, source_target_pairs={{0,1},{1,2},{2,3},{3,4},{4,5},{5,6},{6,7},{7,8},{8,9},{9,10},{10,1... | collective-permute-start | bytes 14155784 | tf_op jit(solution)/shard_map/ppermute | solution.py:84
  487.2 145.1 %collective-permute-start.6 = (bf16[384,48,128]{0,1,2:T(8,128)(2,1)S(1)}, bf16[384,48,128]{0,1,2:T(8,128)(2,1)S(1)}, u32[]{:S(2)}, u32[]{:S(2)}) collective-permute-start(bf16[384,48,128]{0,1,2:T(8,128)(2,1)S(1)} %collective-permute-done.4), channel_id=1, source_target_pairs={{0,15},{1,0},{2,1},{3,2},{4,3},{5,4},{6,5},{7,6},{8,7},{9,8},{10,9... | collective-permute-start | bytes 14155784 | tf_op jit(solution)/shard_map/ppermute | solution.py:86
  491.9 140.5 %copy-start.18 = (bf16[384,48,128]{0,1,2:T(8,128)(2,1)}, bf16[384,48,128]{0,1,2:T(8,128)(2,1)S(1)}, u32[]{:S(2)}) copy-start(bf16[384,48,128]{0,1,2:T(8,128)(2,1)S(1)} %collective-permute-done.7) | copy-start | bytes 14155780
  491.9 148.1 %collective-permute-start.9 = (bf16[384,48,128]{0,1,2:T(8,128)(2,1)S(1)}, bf16[384,48,128]{0,1,2:T(8,128)(2,1)}, u32[]{:S(2)}, u32[]{:S(2)}) collective-permute-start(bf16[384,48,128]{0,1,2:T(8,128)(2,1)S(1)} %collective-permute-done.7), channel_id=1, source_target_pairs={{0,1},{1,2},{2,3},{3,4},{4,5},{5,6},{6,7},{7,8},{8,9},{9,10},{10,1... | collective-permute-start | bytes 14155784 | tf_op jit(solution)/shard_map/ppermute | solution.py:84
  632.3 53.4 %collective-permute-start.8 = (bf16[384,48,128]{0,1,2:T(8,128)(2,1)S(1)}, bf16[384,48,128]{0,1,2:T(8,128)(2,1)}, u32[]{:S(2)}, u32[]{:S(2)}) collective-permute-start(bf16[384,48,128]{0,1,2:T(8,128)(2,1)S(1)} %collective-permute-done.6), channel_id=1, source_target_pairs={{0,15},{1,0},{2,1},{3,2},{4,3},{5,4},{6,5},{7,6},{8,7},{9,8},{10,9... | collective-permute-start | bytes 14155784 | tf_op jit(solution)/shard_map/ppermute | solution.py:86
  640.0 57.7 %collective-permute-start.11 = (bf16[384,48,128]{0,1,2:T(8,128)(2,1)}, bf16[384,48,128]{0,1,2:T(8,128)(2,1)}, u32[]{:S(2)}, u32[]{:S(2)}) collective-permute-start(bf16[384,48,128]{0,1,2:T(8,128)(2,1)} %collective-permute-done.9), channel_id=1, source_target_pairs={{0,1},{1,2},{2,3},{3,4},{4,5},{5,6},{6,7},{7,8},{8,9},{9,10},{10,1... | collective-permute-start | bytes 14155784 | tf_op jit(solution)/shard_map/ppermute | solution.py:84
  685.8 201.4 %collective-permute-start.10 = (bf16[384,48,128]{0,1,2:T(8,128)(2,1)}, bf16[384,48,128]{0,1,2:T(8,128)(2,1)}, u32[]{:S(2)}, u32[]{:S(2)}) collective-permute-start(bf16[384,48,128]{0,1,2:T(8,128)(2,1)} %collective-permute-done.8), channel_id=1, source_target_pairs={{0,15},{1,0},{2,1},{3,2},{4,3},{5,4},{6,5},{7,6},{8,7},{9,8},{10,9... | collective-permute-start | bytes 14155784 | tf_op jit(solution)/shard_map/ppermute | solution.py:86
  697.7 197.2 %collective-permute-start.13 = (bf16[384,48,128]{0,1,2:T(8,128)(2,1)}, bf16[384,48,128]{0,1,2:T(8,128)(2,1)}, u32[]{:S(2)}, u32[]{:S(2)}) collective-permute-start(bf16[384,48,128]{0,1,2:T(8,128)(2,1)} %collective-permute-done.11), channel_id=1, source_target_pairs={{0,1},{1,2},{2,3},{3,4},{4,5},{5,6},{6,7},{7,8},{8,9},{9,10},{10,1... | collective-permute-start | bytes 14155784 | tf_op jit(solution)/shard_map/ppermute | solution.py:84
  855.0 15.8 %slice-start.4 = ((s8[4718592]{0:T(1024)(128)(4,1)}), s8[4194304]{0:T(1024)(128)(4,1)S(1)}, s32[]{:S(2)}) async-start(s8[4718592]{0:T(1024)(128)(4,1)} %bitcast.65), calls=%async_computation.7 | async-start | bytes 8388608
  887.2 65.3 %collective-permute-start.12 = (bf16[384,48,128]{0,1,2:T(8,128)(2,1)}, bf16[384,48,128]{0,1,2:T(8,128)(2,1)S(1)}, u32[]{:S(2)}, u32[]{:S(2)}) collective-permute-start(bf16[384,48,128]{0,1,2:T(8,128)(2,1)} %collective-permute-done.10), channel_id=1, source_target_pairs={{0,15},{1,0},{2,1},{3,2},{4,3},{5,4},{6,5},{7,6},{8,7},{9,8},{10,9... | collective-permute-start | bytes 14155784 | tf_op jit(solution)/shard_map/ppermute | solution.py:86
  894.9 71.6 %collective-permute-start.14 = (bf16[384,48,128]{0,1,2:T(8,128)(2,1)}, bf16[384,48,128]{0,1,2:T(8,128)(2,1)}, u32[]{:S(2)}, u32[]{:S(2)}) collective-permute-start(bf16[384,48,128]{0,1,2:T(8,128)(2,1)} %collective-permute-done.13), channel_id=1, source_target_pairs={{0,1},{1,2},{2,3},{3,4},{4,5},{5,6},{6,7},{7,8},{8,9},{9,10},{10,1... | collective-permute-start | bytes 14155784 | tf_op jit(solution)/shard_map/ppermute | solution.py:84
  1208.9 17.8 %copy-start.1 = (bf16[128,512]{1,0:T(8,128)(2,1)S(1)}, bf16[128,512]{1,0:T(8,128)(2,1)}, u32[]{:S(2)}) copy-start(bf16[128,512]{1,0:T(8,128)(2,1)} %param.14) | copy-start | bytes 393220
  (29 other events, 235.5 us)
Sparse Core Ops, SparseCore 0:
  67.0 120.5 all-gather.2
  1042.3 166.5 all-gather.4
